TPU v7x, 32 devices: a whole 2x2x4 slice. The times are simulated.
32 devices in a mesh: group: 4 (over x, core), tensor: 8 (over z, y).
Axes of the slice: x: 2, y: 2, z: 4, core: 2. Of those that a mesh axis runs over, the one named last changes fastest.
Arguments:
- tokens: bfloat16 [128, 3, 8192], P(('group', 'tensor')), may hold values from -6 to 6
- norm_gain: float32 [8192], replicated, may hold values from 0.25 to 1.75
- w_qkv: bfloat16 [8192, 10240], P(None, 'tensor'), may hold values from -0.0625 to 0.0625
- w_out: bfloat16 [8192, 8192], P('tensor'), may hold values from -0.0625 to 0.0625
- lengths: int32 [32, 4], P(('group', 'tensor')), may hold values from 1 to 512, 1024 in all within a row
- migrate: int32 [32, 4], P(('group', 'tensor')), may hold values from 0 to 3, as said below
- page_order: int32 [32, 12], P(('group', 'tensor')), may hold values from 0 to 11, each once within a row
- kv_pool: bfloat16 [32, 12, 2, 8, 128, 128], P(('group', 'tensor')), as said below
Outputs:
- mixed: bfloat16 [128, 3, 8192], P(('group', 'tensor'))
Inputs may be any that keep to these rules, and one draw needn't show every extreme that they name: `migrate`: on each device every group number is named by exactly 1 row. The 4 lengths of one device sum to 1024. `kv_pool`: cached keys and values of order one or more.
All inputs are finite; a program needn't handle non-finite values.
Results may differ from a plain program's by a relative error of at most 0.013.
Values may be sent and summed in bfloat16 or wider, within the bound.
No kernel may reach another device: no remote copies, remote signals or barrier semaphores. Data moves between devices by JAX's collectives and lax.ppermute only.
A program may use at most 128 MiB of HBM per device.

v0:
```python
import jax
import jax.numpy as jnp
from jax import lax
from jax.sharding import PartitionSpec as P

HEADS = 64
KV_HEADS = 8
HEAD_DIM = 128
PAGE = 128
MAX_PAGES = 4
EPS = 1e-05
ROPE_BASE = 500000.0
NEG_FILL = -1e30


def rotate(values, positions):
    half_dim = values.shape[-1] // 2
    inverse = ROPE_BASE ** (-(jnp.arange(half_dim, dtype=jnp.float32) * 2.0 / values.shape[-1]))
    angles = positions.astype(jnp.float32)[..., None] * inverse
    cosine = jnp.cos(angles)[..., None, :]
    sine = jnp.sin(angles)[..., None, :]
    lower_half = values[..., :half_dim]
    upper_half = values[..., half_dim:]
    return jnp.concatenate(
        [lower_half * cosine - upper_half * sine, upper_half * cosine + lower_half * sine], axis=-1
    )


def cache_stats(queries, pages, row_lens):
    row_total, steps_here, head_count, head_dim = queries.shape
    page_count = pages.shape[1]
    kv_heads = pages.shape[3]
    page_len = pages.shape[4]
    grouped = queries.reshape(row_total, steps_here, kv_heads, head_count // kv_heads, head_dim)
    scores = jnp.einsum(
        "rskgd,rbktd->rskgbt", grouped, pages[:, :, 0], preferred_element_type=jnp.float32
    ) * head_dim ** (-0.5)
    places = (
        jnp.arange(page_count, dtype=jnp.int32)[:, None] * page_len
        + jnp.arange(page_len, dtype=jnp.int32)[None, :]
    )
    inside = (places[None] < row_lens[:, None, None])[:, None, None, None]
    page_top = jnp.max(jnp.where(inside, scores, NEG_FILL), axis=-1)
    weights = jnp.where(inside, jnp.exp(scores - page_top[..., None]), 0.0).astype(jnp.bfloat16)
    page_total = jnp.sum(weights.astype(jnp.float32), axis=-1)
    page_acc = jnp.einsum(
        "rskgbt,rbktd->rskgbd", weights, pages[:, :, 1], preferred_element_type=jnp.float32
    )
    top_score = jnp.max(page_top, axis=-1)
    page_scale = jnp.exp(page_top - top_score[..., None])
    return (
        top_score,
        jnp.sum(page_scale * page_total, axis=-1),
        jnp.sum(page_scale[..., None] * page_acc, axis=-2),
    )


def finish(queries, cache_parts, all_keys, all_values):
    row_total, steps_here, head_count, head_dim = queries.shape
    kv_heads = all_keys.shape[2]
    grouped = queries.reshape(row_total, steps_here, kv_heads, head_count // kv_heads, head_dim)
    scores = jnp.einsum(
        "rskgd,rukd->rskgu", grouped, all_keys, preferred_element_type=jnp.float32
    ) * head_dim ** (-0.5)
    allowed = jnp.arange(all_keys.shape[1])[None, :] <= jnp.arange(steps_here)[:, None]
    allowed = allowed[None, :, None, None, :]
    new_top = jnp.max(jnp.where(allowed, scores, NEG_FILL), axis=-1)
    weights = jnp.where(allowed, jnp.exp(scores - new_top[..., None]), 0.0).astype(jnp.bfloat16)
    new_total = jnp.sum(weights.astype(jnp.float32), axis=-1)
    new_acc = jnp.einsum(
        "rskgu,rukd->rskgd", weights, all_values, preferred_element_type=jnp.float32
    )
    cache_top, cache_total, cache_acc = cache_parts
    top_score = jnp.maximum(cache_top, new_top)
    cache_scale = jnp.exp(cache_top - top_score)
    new_scale = jnp.exp(new_top - top_score)
    merged = (cache_scale[..., None] * cache_acc + new_scale[..., None] * new_acc) / (
        cache_scale * cache_total + new_scale * new_total
    )[..., None]
    return merged.reshape(row_total, steps_here, head_count * head_dim).astype(jnp.bfloat16)


def per_device(tokens, norm_gain, w_qkv, w_out, lengths, migrate, page_order, kv_pool):
    row_lens = lengths[0]
    destinations = migrate[0]
    pool_order = page_order[0]
    page_pool = kv_pool[0]
    row_total = row_lens.shape[0]
    pool_size = page_pool.shape[0]
    slot_ids = jnp.arange(row_total, dtype=jnp.int32)
    sort_keys = destinations * row_total + slot_ids
    row_ranks = jnp.sum((sort_keys[None, :] < sort_keys[:, None]).astype(jnp.int32), axis=1)
    placing = row_ranks[:, None] == slot_ids[None, :]
    pages_used = (row_lens + PAGE - 1) // PAGE
    offsets = jnp.cumsum(pages_used) - pages_used
    sorted_lens = jnp.sum(jnp.where(placing, row_lens[:, None], 0), axis=0)
    sorted_first = jnp.sum(jnp.where(placing, offsets[:, None], 0), axis=0)
    page_slots = jnp.clip(
        sorted_first[:, None] + jnp.arange(MAX_PAGES, dtype=jnp.int32)[None, :], 0, pool_size - 1
    )
    home_pages = page_pool[pool_order[page_slots]]
    new_lens = lax.all_to_all(sorted_lens, "group", split_axis=0, concat_axis=0, tiled=True)
    moved_pages = lax.all_to_all(home_pages, "group", split_axis=0, concat_axis=0, tiled=True)
    width_q = HEADS * HEAD_DIM
    width_k = KV_HEADS * HEAD_DIM
    keys_so_far = jnp.zeros((row_total, 0, KV_HEADS, HEAD_DIM), jnp.bfloat16)
    values_so_far = jnp.zeros((row_total, 0, KV_HEADS, HEAD_DIM), jnp.bfloat16)
    steps_here = tokens.shape[1]
    floats = tokens.astype(jnp.float32)
    normed = (
        floats * lax.rsqrt(jnp.mean(floats * floats, axis=-1, keepdims=True) + EPS) * norm_gain
    ).astype(jnp.bfloat16)
    gathered = jnp.einsum(
        "rsd,dc->rsc",
        lax.all_gather(normed, "tensor", axis=0, tiled=True),
        w_qkv,
        preferred_element_type=jnp.float32,
    ).astype(jnp.bfloat16)
    full_rows = lax.all_to_all(gathered, "tensor", split_axis=0, concat_axis=2, tiled=True)
    positions = new_lens[:, None] + 0 + jnp.arange(steps_here, dtype=jnp.int32)[None, :]
    queries = rotate(
        full_rows[..., :width_q]
        .reshape(row_total, steps_here, HEADS, HEAD_DIM)
        .astype(jnp.float32),
        positions,
    ).astype(jnp.bfloat16)
    keys_here = rotate(
        full_rows[..., width_q : width_q + width_k]
        .reshape(row_total, steps_here, KV_HEADS, HEAD_DIM)
        .astype(jnp.float32),
        positions,
    ).astype(jnp.bfloat16)
    values_here = full_rows[..., width_q + width_k :].reshape(
        row_total, steps_here, KV_HEADS, HEAD_DIM
    )
    all_keys = jnp.concatenate([keys_so_far, keys_here], axis=1)
    all_values = jnp.concatenate([values_so_far, values_here], axis=1)
    attended = finish(queries, cache_stats(queries, moved_pages, new_lens), all_keys, all_values)
    spread = lax.all_to_all(attended, "tensor", split_axis=2, concat_axis=0, tiled=True)
    summed = lax.psum_scatter(
        jnp.einsum("rsc,cd->rsd", spread, w_out, preferred_element_type=jnp.float32).astype(
            jnp.bfloat16
        ),
        "tensor",
        scatter_dimension=0,
        tiled=True,
    ).astype(jnp.float32)
    output = (floats + summed).astype(jnp.bfloat16)
    return output


def solution(mesh):
    in_specs = (
        P(("group", "tensor"), None, None),
        P(),
        P(None, "tensor"),
        P("tensor", None),
        P(("group", "tensor"), None),
        P(("group", "tensor"), None),
        P(("group", "tensor"), None),
        P(("group", "tensor"), None, None, None, None, None),
    )
    out_specs = P(("group", "tensor"), None, None)
    return jax.shard_map(
        per_device, mesh=mesh, in_specs=in_specs, out_specs=out_specs, check_vma=False
    )
```

profile of v0, /device:TPU:0, one launch (start us, length us, event | category | flops | bytes accessed | tf_op | source)
XLA Modules:
  0.0 357.1 jit_solution(14385449491544345333)
XLA Ops:
  6.5 0.0 all-gather.2.cloned.1.call-start
  6.5 1.1 fusion.25
  7.7 1.1 fusion.27
  8.8 0.9 copy.104
  9.7 0.0 all-gather.2.cloned.1.call-update
  9.7 0.7 and_select_fusion.1
  10.4 0.2 reduce-window.8
  10.6 0.7 add_bitcast_fusion
  11.2 0.7 bitcast_add_fusion
  11.9 0.2 convert_reduce_fusion.2
  12.1 0.7 bitcast_subtract_fusion.1
  12.7 0.7 select_reduce_fusion.2
  13.5 0.7 copy.101
  14.1 4.2 %all-to-all-start = ((s32[4,1,1]{2,1,0:T(1,128)}), s32[4,1,1]{2,1,0:T(1,128)S(1)}, u32[]{:S(2)}, u32[]{:S(2)}) async-start(s32[4,1,1]{2,1,0:T(1,128)} %copy.101), calls=%async_computation | async-start | bytes 4096 | tf_op jit(solution)/shard_map/all_to_all | solution.py:102
  18.4 0.1 compare_select_fusion.1
  18.5 0.1 reshape.288
  18.5 43.2 %all-gather.2.cloned.1.call-done = bf16[32,3,8192]{2,1,0:T(4,128)(2,1)} async-done(((bf16[4,3,8192]{2,1,0:T(4,128)(2,1)}), bf16[32,3,8192]{2,1,0:T(4,128)(2,1)}) %all-gather.2.cloned.1.call-update) | async-done | bytes 1572880 | tf_op jit(solution)/shard_map/all_gather | solution.py:115
  61.7 12.2 %fusion.9 = bf16[32,3,1280]{2,0,1:T(8,128)(2,1)S(1)} fusion(bf16[8192,1280]{1,0:T(8,128)(2,1)} %param.10, bf16[32,3,8192]{2,1,0:T(4,128)(2,1)} %all-gather.2.cloned.1.call-done), kind=kOutput, calls=%fused_computation.11 | convolution fusion | flops 2013388800 | bytes 22790144 | tf_op jit(solution)/shard_map/rsd,dc->rsc/dot_general | solution.py:113
  73.9 0.9 copy.106
  74.8 0.0 all-to-all-done
  74.8 3.4 all-to-all-start.2
  78.3 0.0 copy-done
  78.3 0.7 gather_fusion
  79.0 0.1 gather.9
  79.1 0.1 reshape.296
  79.2 7.5 %gather_fusion.1 = bf16[16,2,8,128,128]{4,3,2,1,0:T(8,128)(2,1)} fusion(bf16[12,2,8,128,128]{4,3,2,1,0:T(8,128)(2,1)} %bitcast.134, s32[1024]{0:T(1024)S(1)} %pad_clamp_fusion), kind=kCustom, calls=%fused_computation.1 | custom fusion | bytes 16777280 | tf_op jit(solution)/shard_map/gather | solution.py:101
  86.7 10.3 %copy.102 = bf16[4,4,2,8,128,128]{5,4,1,3,2,0:T(8,128)(2,1)} copy(bf16[4,4,2,8,128,128]{5,4,3,2,1,0:T(8,128)(2,1)} %bitcast.131) | data formatting | bytes 16777216 | tf_op jit(solution)/shard_map/gather | solution.py:101
  97.0 0.0 all-to-all-done.2
  97.0 5.7 %all-to-all-start.1 = ((bf16[4,4,2,8,128,128]{5,4,1,3,2,0:T(8,128)(2,1)}), bf16[4,4,2,8,128,128]{5,4,1,3,2,0:T(8,128)(2,1)}, u32[]{:S(2)}, u32[]{:S(2)}) async-start(bf16[4,4,2,8,128,128]{5,4,1,3,2,0:T(8,128)(2,1)} %copy.102), calls=%async_computation.1 | async-start | bytes 16777216 | tf_op jit(solution)/shard_map/all_to_all | solution.py:103
  102.8 0.2 all-reduce.3.cloned.1.call-start
  103.0 0.1 iota_add_fusion
  103.1 0.2 reduce.1
  103.3 0.1 add_convert_fusion.1
  103.3 0.1 multiply_cosine_fusion
  103.5 0.1 broadcast_compare_fusion
  103.6 0.1 copy.174
  103.7 0.2 all_to_all.41
  103.9 0.3 reshape.284
  104.2 0.1 fusion.48
  104.3 0.1 fusion.35
  104.4 0.2 fusion.29
  104.6 0.8 select_reduce_fusion
  105.4 0.2 convert_reduce_fusion.1
  105.7 90.2 %all-to-all-done.1 = bf16[4,4,2,8,128,128]{5,4,1,3,2,0:T(8,128)(2,1)} async-done(((bf16[4,4,2,8,128,128]{5,4,1,3,2,0:T(8,128)(2,1)}), bf16[4,4,2,8,128,128]{5,4,1,3,2,0:T(8,128)(2,1)}, u32[]{:S(2)}, u32[]{:S(2)}) %all-to-all-start.1) | async-done | bytes 8388640 | tf_op jit(solution)/shard_map/all_to_all | solution.py:103
  195.9 3.6 %fusion.17 = (f32[4,3,8,8,4]{3,1,4,2,0:T(4,128)S(1)}, f32[4,8,4,128,3,8]{3,5,4,2,1,0:T(8,128)S(1)}) fusion(pred[4,4,128]{2,1,0:T(4,128)(4,1)S(1)} %broadcast_compare_fusion, bf16[4,4,2,8,128,128]{5,4,1,3,2,0:T(8,128)(2,1)} %all-to-all-done.1, bf16[4,3,8,8,64]{4,3,2,0,1:T(8,128)(2,1)S(1)} %get-tuple-element.15, ...), kind=kOutput, calls=%fused_computation.21 | convolution fusion | flops 102233088 | bytes 5978112 | tf_op jit(solution)/shard_map/rskgd,rbktd->rskgbt/dot_general | solution.py:35
  199.5 1.2 convert_reduce_fusion
  200.7 0.2 multiply_reduce_fusion
  200.9 0.1 multiply_add_fusion
  201.0 3.6 fusion.12
  204.5 0.6 fusion.23
  205.2 6.5 %copy.134 = bf16[4,3,8,8,128]{0,1,4,3,2:T(4,128)(2,1)} copy(bf16[4,3,8,8,128]{4,3,1,2,0:T(8,128)(2,1)S(1)} %fusion.23) | data formatting | bytes 393216 | tf_op jit(solution)/shard_map/convert_element_type | solution.py:80
  211.7 9.7 %reshape.316 = bf16[8,2,6144]{2,1,0:T(2,128)(2,1)S(1)} reshape(bf16[8192,3,4]{2,1,0:T(4,128)(2,1)} %bitcast.132) | data formatting | bytes 393216
  221.4 13.5 %all_to_all.50 = bf16[8,2,6144]{2,1,0:T(2,128)(2,1)S(1)} all-to-all(bf16[8,2,6144]{2,1,0:T(2,128)(2,1)S(1)} %reshape.316), channel_id=1, replica_groups=mesh['group'=4,'tensor'=8] {'tensor'}, dimensions={0} | all-to-all | bytes 393216 | tf_op jit(solution)/shard_map/all_to_all | solution.py:139
  234.9 8.5 %reshape.317 = bf16[8192,3,4]{2,1,0:T(4,128)(2,1)} reshape(bf16[8,2,6144]{2,1,0:T(2,128)(2,1)S(1)} %all_to_all.50) | data formatting | bytes 393216
  243.4 7.9 %copy.135 = bf16[4,3,8,1024]{3,2,0,1:T(8,128)(2,1)S(1)} copy(bf16[4,3,8,1024]{0,1,3,2:T(4,128)(2,1)} %bitcast.133) | data formatting | bytes 393216 | tf_op jit(solution)/shard_map/all_to_all | solution.py:139
  251.3 0.2 copy.121
  251.5 0.1 all_to_all.45
  251.5 0.0 copy-start.1
  251.6 9.7 %fusion.4 = bf16[32,3,8192]{2,0,1:T(8,128)(2,1)} fusion(bf16[32,3,1024]{2,0,1:T(8,128)(2,1)S(1)} %all_to_all.45, bf16[1024,8192]{1,0:T(8,128)(2,1)} %param.11), kind=kOutput, calls=%fused_computation.6 | convolution fusion | flops 1611399168 | bytes 18546688 | tf_op jit(solution)/shard_map/rsc,cd->rsd/dot_general | solution.py:141
  261.3 0.0 all-reduce.3.cloned.1.call-update
  261.3 0.6 copy-done.3
  261.9 0.6 dynamic-slice
  263.2 85.3 %all-reduce.3.cloned.1.call-done = bf16[32,3,8192]{2,0,1:T(8,128)(2,1)} async-done(((bf16[32,3,8192]{2,0,1:T(8,128)(2,1)}), bf16[32,3,8192]{2,0,1:T(8,128)(2,1)}) %all-reduce.3.cloned.1.call-update) | async-done | bytes 1572880
  348.4 1.8 fusion.28
  (18 shorter events, 0.1 us)
Async XLA Ops:
  6.5 71.8 %copy-start = (s32[1,12]{1,0:T(1,128)S(1)}, s32[1,12]{1,0:T(1,128)}, u32[]{:S(2)}) copy-start(s32[1,12]{1,0:T(1,128)} %param.14) | copy-start | bytes 148
  6.5 55.2 %all-gather.2.cloned.1.call-start = ((), (), s32[]{:S(2)}) async-start(), calls=%async_computation.4 | async-start | bytes 2359296 | tf_op jit(solution)/shard_map/all_gather | solution.py:115
  14.1 60.7 %all-to-all-start = ((s32[4,1,1]{2,1,0:T(1,128)}), s32[4,1,1]{2,1,0:T(1,128)S(1)}, u32[]{:S(2)}, u32[]{:S(2)}) async-start(s32[4,1,1]{2,1,0:T(1,128)} %copy.101), calls=%async_computation | async-start | bytes 4096 | tf_op jit(solution)/shard_map/all_to_all | solution.py:102
  74.8 22.2 %all-to-all-start.2 = ((bf16[32,3,1280]{2,1,0:T(4,128)(2,1)}), bf16[32,3,1280]{2,1,0:T(4,128)(2,1)S(1)}, u32[]{:S(2)}, u32[]{:S(2)}) async-start(bf16[32,3,1280]{2,1,0:T(4,128)(2,1)} %copy.106), calls=%async_computation.2 | async-start | bytes 655360 | tf_op jit(solution)/shard_map/all_to_all | solution.py:119
  97.0 98.8 %all-to-all-start.1 = ((bf16[4,4,2,8,128,128]{5,4,1,3,2,0:T(8,128)(2,1)}), bf16[4,4,2,8,128,128]{5,4,1,3,2,0:T(8,128)(2,1)}, u32[]{:S(2)}, u32[]{:S(2)}) async-start(bf16[4,4,2,8,128,128]{5,4,1,3,2,0:T(8,128)(2,1)} %copy.102), calls=%async_computation.1 | async-start | bytes 16777216 | tf_op jit(solution)/shard_map/all_to_all | solution.py:103
  102.8 245.7 %all-reduce.3.cloned.1.call-start = ((), (), s32[]{:S(2)}) async-start(), calls=%async_computation.5 | async-start | bytes 3145728
  251.5 98.7 %copy-start.1 = (s32[1,12]{1,0:T(1,128)S(1)}, s32[1,12]{1,0:T(1,128)}, u32[]{:S(2)}) copy-start(s32[1,12]{1,0:T(1,128)} %param.14) | copy-start | bytes 148
  261.3 0.7 copy-start.3
  261.3 87.2 %copy-start.2 = (bf16[4,3,8192]{2,0,1:T(4,128)(2,1)S(1)}, bf16[4,3,8192]{2,0,1:T(4,128)(2,1)}, u32[]{:S(2)}) copy-start(bf16[4,3,8192]{2,0,1:T(4,128)(2,1)} %param.8) | copy-start | bytes 589828
Sparse Core Ops, SparseCore 0:
  9.8 51.8 all-gather.1
  261.4 86.9 all-reduce.2
where the time goes:
time: 358 us; the launch traced here: 357 us
  waiting for transfers between devices  219 us (61%)
  local copies, waits for them, and re-layouts  56 us (16%)
  matrix products  30.5 us (9%)
  between operations  14.3 us (4%)
  starting transfers between devices  13.6 us (4%)
  blocking collectives  13.5 us (4%)
  other arithmetic  10.5 us (3%)
    all_to_all x1, waiting for transfers between devices, per_device(): lax.all_to_all(home_pages, 'group', split_axis=0, concat_axis=0, tiled=True)  90.2 us
    unnamed x3, waiting for transfers between devices  85.3 us
    all_gather x1, waiting for transfers between devices, per_device(): lax.all_gather(normed, 'tensor', axis=0, tiled=True)  43.2 us
    unnamed x11, local copies, waits for them, and re-layouts  19.4 us
    gather x4, local copies, waits for them, and re-layouts, per_device(): home_pages = page_pool[pool_order[page_slots]]  18.6 us
    all_to_all x1, blocking collectives, per_device(): lax.all_to_all(attended, 'tensor', split_axis=2, concat_axis=0, tiled=True)  13.5 us
    dot_general x1, matrix products, per_device(): jnp.einsum('rsd,dc->rsc', lax.all_gather(normed, 'tensor', axis=0, tiled=...  12.2 us
    dot_general x1, matrix products, per_device(): jnp.einsum('rsc,cd->rsd', spread, w_out, preferred_element_type=jnp.float32)  9.71 us
  transfers between devices with their start and end apart: 5, of which 3 were waited for; matrix products, arithmetic and copies ran while one was open for 11% of the time, Pallas kernels for 0%

commit v1 on v0

--- a/solution.py
+++ b/solution.py
@@ -136,7 +136,12 @@
     all_keys = jnp.concatenate([keys_so_far, keys_here], axis=1)
     all_values = jnp.concatenate([values_so_far, values_here], axis=1)
     attended = finish(queries, cache_stats(queries, moved_pages, new_lens), all_keys, all_values)
-    spread = lax.all_to_all(attended, "tensor", split_axis=2, concat_axis=0, tiled=True)
+    spread = jnp.concatenate(
+        lax.all_to_all(
+            jnp.stack(jnp.split(attended, lax.axis_size("tensor"), axis=2)), "tensor", 0, 0
+        ),
+        axis=0,
+    )
     summed = lax.psum_scatter(
         jnp.einsum("rsc,cd->rsd", spread, w_out, preferred_element_type=jnp.float32).astype(
             jnp.bfloat16

time: 358 us -> 325 us (0.908)
  local copies, waits for them, and re-layouts: 56 us -> 23.5 us
    unnamed x11 -> x16, local copies, waits for them, and re-layouts: 19.4 us -> 1.35 us
    all_to_all x3 -> x1, local copies, waits for them, and re-layouts: 8.09 us -> 0.07 us  [per_device(): lax.all_to_all(jnp.stack(jnp.split(attended, lax.axis_size('tensor'), axi...]
    convert_element_type x1 -> x2, local copies, waits for them, and re-layouts: 6.53 us -> 0.09 us  [finish(): merged.reshape(row_total, steps_here, head_count * head_dim)]
  transfers between devices with their start and end apart: 5 -> 5, of which waited for: 3 -> 3; matrix products, arithmetic and copies ran while one was open for 11% -> 12% of each run, Pallas kernels for 0% -> 0%
where the time goes in v1:
time: 325 us
  waiting for transfers between devices  219 us (67%)
  matrix products  30.5 us (9%)
  local copies, waits for them, and re-layouts  23.5 us (7%)
  between operations  14.3 us (4%)
  starting transfers between devices  13.6 us (4%)
  blocking collectives  13.5 us (4%)
  other arithmetic  10.5 us (3%)
    all_to_all x1, waiting for transfers between devices, per_device(): lax.all_to_all(home_pages, 'group', split_axis=0, concat_axis=0, tiled=True)  90.2 us
    unnamed x3, waiting for transfers between devices  85.3 us
    all_gather x1, waiting for transfers between devices, per_device(): lax.all_gather(normed, 'tensor', axis=0, tiled=True)  43.2 us
    gather x4, local copies, waits for them, and re-layouts, per_device(): home_pages = page_pool[pool_order[page_slots]]  18.6 us
    all_to_all x1, blocking collectives, per_device(): lax.all_to_all(jnp.stack(jnp.split(attended, lax.axis_size('tensor'), axi...  13.5 us
    dot_general x1, matrix products, per_device(): jnp.einsum('rsd,dc->rsc', lax.all_gather(normed, 'tensor', axis=0, tiled=...  12.2 us
    dot_general x1, matrix products, per_device(): jnp.einsum('rsc,cd->rsd', spread, w_out, preferred_element_type=jnp.float32)  9.71 us
  transfers between devices with their start and end apart: 5, of which 3 were waited for; matrix products, arithmetic and copies ran while one was open for 12% of the time, Pallas kernels for 0%

profile of v1, /device:TPU:0, one launch (start us, length us, event | category | flops | bytes accessed | tf_op | source)
XLA Modules:
  0.0 324.6 jit_solution(14657102957977391440)
XLA Ops:
  6.5 0.0 copy-start
  6.5 0.0 all-gather.2.cloned.1.call-start
  6.5 1.1 fusion.25
  7.7 1.1 fusion.27
  8.8 0.9 copy.105
  9.7 0.0 all-gather.2.cloned.1.call-update
  9.7 0.7 and_select_fusion.1
  10.4 0.2 reduce-window.8
  10.6 0.7 add_bitcast_fusion
  11.2 0.7 bitcast_add_fusion
  11.9 0.2 convert_reduce_fusion.2
  12.1 0.7 bitcast_subtract_fusion.1
  12.7 0.7 select_reduce_fusion.2
  13.5 0.7 copy.102
  14.1 4.2 %all-to-all-start = ((s32[4,1,1]{2,1,0:T(1,128)}), s32[4,1,1]{2,1,0:T(1,128)S(1)}, u32[]{:S(2)}, u32[]{:S(2)}) async-start(s32[4,1,1]{2,1,0:T(1,128)} %copy.102), calls=%async_computation | async-start | bytes 4096 | tf_op jit(solution)/shard_map/all_to_all | solution.py:102
  18.4 0.1 compare_select_fusion.1
  18.5 0.1 reshape.292
  18.5 43.2 %all-gather.2.cloned.1.call-done = bf16[32,3,8192]{2,1,0:T(4,128)(2,1)} async-done(((bf16[4,3,8192]{2,1,0:T(4,128)(2,1)}), bf16[32,3,8192]{2,1,0:T(4,128)(2,1)}) %all-gather.2.cloned.1.call-update) | async-done | bytes 1572880 | tf_op jit(solution)/shard_map/all_gather | solution.py:115
  61.7 12.2 %fusion.9 = bf16[32,3,1280]{2,0,1:T(8,128)(2,1)S(1)} fusion(bf16[8192,1280]{1,0:T(8,128)(2,1)} %param.10, bf16[32,3,8192]{2,1,0:T(4,128)(2,1)} %all-gather.2.cloned.1.call-done), kind=kOutput, calls=%fused_computation.11 | convolution fusion | flops 2013388800 | bytes 22790144 | tf_op jit(solution)/shard_map/rsd,dc->rsc/dot_general | solution.py:113
  73.9 0.9 copy.107
  74.8 0.0 all-to-all-done
  74.8 3.4 %all-to-all-start.2 = ((bf16[32,3,1280]{2,1,0:T(4,128)(2,1)}), bf16[32,3,1280]{2,1,0:T(4,128)(2,1)S(1)}, u32[]{:S(2)}, u32[]{:S(2)}) async-start(bf16[32,3,1280]{2,1,0:T(4,128)(2,1)} %copy.107), calls=%async_computation.2 | async-start | bytes 655360 | tf_op jit(solution)/shard_map/all_to_all | solution.py:119
  78.3 0.0 copy-done
  78.3 0.7 gather_fusion
  79.0 0.1 gather.9
  79.1 0.1 reshape.300
  79.2 7.5 %gather_fusion.1 = bf16[16,2,8,128,128]{4,3,2,1,0:T(8,128)(2,1)} fusion(bf16[12,2,8,128,128]{4,3,2,1,0:T(8,128)(2,1)} %bitcast.163, s32[1024]{0:T(1024)S(1)} %pad_clamp_fusion), kind=kCustom, calls=%fused_computation.1 | custom fusion | bytes 16777280 | tf_op jit(solution)/shard_map/gather | solution.py:101
  86.7 10.3 %copy.103 = bf16[4,4,2,8,128,128]{5,4,1,3,2,0:T(8,128)(2,1)} copy(bf16[4,4,2,8,128,128]{5,4,3,2,1,0:T(8,128)(2,1)} %bitcast.162) | data formatting | bytes 16777216 | tf_op jit(solution)/shard_map/gather | solution.py:101
  97.0 0.0 all-to-all-done.2
  97.0 5.7 %all-to-all-start.1 = ((bf16[4,4,2,8,128,128]{5,4,1,3,2,0:T(8,128)(2,1)}), bf16[4,4,2,8,128,128]{5,4,1,3,2,0:T(8,128)(2,1)}, u32[]{:S(2)}, u32[]{:S(2)}) async-start(bf16[4,4,2,8,128,128]{5,4,1,3,2,0:T(8,128)(2,1)} %copy.103), calls=%async_computation.1 | async-start | bytes 16777216 | tf_op jit(solution)/shard_map/all_to_all | solution.py:103
  102.8 0.2 all-reduce.3.cloned.1.call-start
  103.0 0.1 iota_add_fusion
  103.1 0.2 reduce.1
  103.3 0.1 add_convert_fusion.1
  103.3 0.1 multiply_cosine_fusion
  103.5 0.1 broadcast_compare_fusion
  103.6 0.1 copy.170
  103.7 0.2 all_to_all.31
  103.9 0.3 reshape.288
  104.2 0.1 fusion.56
  104.3 0.1 fusion.35
  104.4 0.2 fusion.29
  104.6 0.8 select_reduce_fusion
  105.4 0.2 convert_reduce_fusion.1
  105.7 90.2 %all-to-all-done.1 = bf16[4,4,2,8,128,128]{5,4,1,3,2,0:T(8,128)(2,1)} async-done(((bf16[4,4,2,8,128,128]{5,4,1,3,2,0:T(8,128)(2,1)}), bf16[4,4,2,8,128,128]{5,4,1,3,2,0:T(8,128)(2,1)}, u32[]{:S(2)}, u32[]{:S(2)}) %all-to-all-start.1) | async-done | bytes 8388640 | tf_op jit(solution)/shard_map/all_to_all | solution.py:103
  195.9 3.6 %fusion.17 = (f32[4,3,8,8,4]{3,1,4,2,0:T(4,128)S(1)}, f32[4,8,4,128,3,8]{3,5,4,2,1,0:T(8,128)S(1)}) fusion(pred[4,4,128]{2,1,0:T(4,128)(4,1)S(1)} %broadcast_compare_fusion, bf16[4,4,2,8,128,128]{5,4,1,3,2,0:T(8,128)(2,1)} %all-to-all-done.1, bf16[4,3,8,8,64]{4,3,2,0,1:T(8,128)(2,1)S(1)} %get-tuple-element.15, ...), kind=kOutput, calls=%fused_computation.21 | convolution fusion | flops 102233088 | bytes 5978112 | tf_op jit(solution)/shard_map/rskgd,rbktd->rskgbt/dot_general | solution.py:35
  199.5 1.2 convert_reduce_fusion
  200.7 0.2 multiply_reduce_fusion
  200.9 0.1 multiply_add_fusion
  201.0 3.6 %fusion.12 = f32[4,3,8,8,128]{4,3,1,2,0:T(8,128)S(1)} fusion(bf16[4,4,2,8,128,128]{5,4,1,3,2,0:T(8,128)(2,1)} %all-to-all-done.1, f32[4,3,8,8,4]{3,1,4,2,0:T(4,128)S(1)} %get-tuple-element.13, f32[4,8,4,128,3,8]{3,5,4,2,1,0:T(8,128)S(1)} %get-tuple-element.25, f32[4,3,8,8,4]{3,1,4,2,0:T(4,128)S(1)} %get-tuple-element.24, ...), kind=kOutput, calls=%fused_computation.13 | convolution fusion | flops 102531072 | bytes 6187008 | tf_op jit(solution)/shard_map/rskgbt,rbktd->rskgbd/dot_general | solution.py:46
  204.5 0.6 fusion.23
  205.2 0.1 convert_element_type.76
  205.4 13.5 %all_to_all.37 = bf16[8,4,3,1024]{3,1,2,0:T(4,128)(2,1)S(1)} all-to-all(bf16[8,4,3,1024]{3,1,2,0:T(4,128)(2,1)S(1)} %fusion.43), channel_id=1, replica_groups=mesh['group'=4,'tensor'=8] {'tensor'}, dimensions={0} | all-to-all | bytes 393216 | tf_op jit(solution)/shard_map/all_to_all | solution.py:140
  219.0 0.1 copy.120
  219.0 0.1 reshape.287
  219.1 0.0 copy-start.1
  219.1 9.7 %fusion.4 = bf16[32,3,8192]{2,0,1:T(8,128)(2,1)} fusion(bf16[32,3,1024]{2,0,1:T(8,128)(2,1)S(1)} %reshape.287, bf16[1024,8192]{1,0:T(8,128)(2,1)} %param.11), kind=kOutput, calls=%fused_computation.6 | convolution fusion | flops 1611399168 | bytes 18546688 | tf_op jit(solution)/shard_map/rsc,cd->rsd/dot_general | solution.py:146
  228.8 0.0 all-reduce.3.cloned.1.call-update
  228.8 0.6 copy-done.3
  229.5 0.6 dynamic-slice
  230.7 85.2 %all-reduce.3.cloned.1.call-done = bf16[32,3,8192]{2,0,1:T(8,128)(2,1)} async-done(((bf16[32,3,8192]{2,0,1:T(8,128)(2,1)}), bf16[32,3,8192]{2,0,1:T(8,128)(2,1)}) %all-reduce.3.cloned.1.call-update) | async-done | bytes 1572880
  316.0 0.0 copy-done.2
  316.0 1.8 fusion.28
  317.8 0.0 copy-done.1
  (24 shorter events, 0.3 us)
Async XLA Ops:
  6.5 71.8 %copy-start = (s32[1,12]{1,0:T(1,128)S(1)}, s32[1,12]{1,0:T(1,128)}, u32[]{:S(2)}) copy-start(s32[1,12]{1,0:T(1,128)} %param.14) | copy-start | bytes 148
  6.5 55.2 %all-gather.2.cloned.1.call-start = ((), (), s32[]{:S(2)}) async-start(), calls=%async_computation.4 | async-start | bytes 2359296 | tf_op jit(solution)/shard_map/all_gather | solution.py:115
  14.1 60.7 %all-to-all-start = ((s32[4,1,1]{2,1,0:T(1,128)}), s32[4,1,1]{2,1,0:T(1,128)S(1)}, u32[]{:S(2)}, u32[]{:S(2)}) async-start(s32[4,1,1]{2,1,0:T(1,128)} %copy.102), calls=%async_computation | async-start | bytes 4096 | tf_op jit(solution)/shard_map/all_to_all | solution.py:102
  74.8 22.2 %all-to-all-start.2 = ((bf16[32,3,1280]{2,1,0:T(4,128)(2,1)}), bf16[32,3,1280]{2,1,0:T(4,128)(2,1)S(1)}, u32[]{:S(2)}, u32[]{:S(2)}) async-start(bf16[32,3,1280]{2,1,0:T(4,128)(2,1)} %copy.107), calls=%async_computation.2 | async-start | bytes 655360 | tf_op jit(solution)/shard_map/all_to_all | solution.py:119
  97.0 98.8 %all-to-all-start.1 = ((bf16[4,4,2,8,128,128]{5,4,1,3,2,0:T(8,128)(2,1)}), bf16[4,4,2,8,128,128]{5,4,1,3,2,0:T(8,128)(2,1)}, u32[]{:S(2)}, u32[]{:S(2)}) async-start(bf16[4,4,2,8,128,128]{5,4,1,3,2,0:T(8,128)(2,1)} %copy.103), calls=%async_computation.1 | async-start | bytes 16777216 | tf_op jit(solution)/shard_map/all_to_all | solution.py:103
  102.8 213.2 %all-reduce.3.cloned.1.call-start = ((), (), s32[]{:S(2)}) async-start(), calls=%async_computation.5 | async-start | bytes 3145728
  219.1 98.7 %copy-start.1 = (s32[1,12]{1,0:T(1,128)S(1)}, s32[1,12]{1,0:T(1,128)}, u32[]{:S(2)}) copy-start(s32[1,12]{1,0:T(1,128)} %param.14) | copy-start | bytes 148
  228.8 0.7 copy-start.3
  228.8 87.1 %copy-start.2 = (bf16[4,3,8192]{2,0,1:T(4,128)(2,1)S(1)}, bf16[4,3,8192]{2,0,1:T(4,128)(2,1)}, u32[]{:S(2)}) copy-start(bf16[4,3,8192]{2,0,1:T(4,128)(2,1)} %param.8) | copy-start | bytes 589828
Sparse Core Ops, SparseCore 0:
  9.8 51.8 all-gather.1
  229.0 86.9 all-reduce.2
